TPU v7x, 32 devices: a whole 2x2x4 slice. The times are simulated.
32 devices in a mesh: rows: 32 (over z, y, x, core).
Axes of the slice: x: 2, y: 2, z: 4, core: 2. Of those that a mesh axis runs over, the one named last changes fastest.
Arguments:
- history: float32 [32, 512, 4096], P(None, 'rows'), may hold values from 0.2 to 1.8, as said below
- source: float32 [512, 4096], P('rows'), may hold values from 0.5 to 2, as said below
- diffusivity: float32 [512, 4096], P('rows'), may hold values from 0.5 to 2, as said below
- target: float32 [512, 4096], P('rows'), may hold values from -0.5 to 2.5, as said below
Outputs:
- update: float32 [512, 4096], P('rows')
- totals: float32 [2], replicated
Inputs may be any that keep to these rules, and one draw needn't show every extreme that they name: `history`: every level is a field between 0.2 and 1.8, smooth with a small cell-by-cell variation. `source`: a positive field between 0.5 and 2. `diffusivity`: a positive field between 0.5 and 2, smooth with a small cell-by-cell variation. `target`: a field between -0.5 and 2.5, smooth with a small cell-by-cell variation.
All inputs are finite; a program needn't handle non-finite values.
Results may differ from a plain program's by a relative error of at most 0.0003.
Values sent between devices are 32-bit elements; how exact they have to be, the bound alone decides.
A program may use at most 128 MiB of HBM per device.

v0:
```python
import jax
import jax.numpy as jnp
from jax import lax
from jax.sharding import PartitionSpec as P

STIFF = 1024


frac_order = 0.6


def memory_weights(levels):
    moments = jnp.arange(levels + 1, dtype=jnp.float32)
    powered = moments ** (1.0 - frac_order)
    decay_terms = powered[1:] - powered[:-1]
    padding = jnp.zeros((1,), jnp.float32)
    return jnp.concatenate([decay_terms[1:], padding]) - jnp.concatenate([padding, decay_terms[1:]])


def take_from(array_in, stride, fill_value, along, before):
    length = array_in.shape[along]
    pad_shape = list(array_in.shape)
    pad_shape[along] = stride
    filler = jnp.full(pad_shape, fill_value, array_in.dtype)
    if before:
        kept = lax.slice_in_dim(array_in, 0, length - stride, 1, along)
        return jnp.concatenate([filler, kept], along)
    kept = lax.slice_in_dim(array_in, stride, length, 1, along)
    return jnp.concatenate([kept, filler], along)


def cyclic_solve(along, sub_diag, main_diag, sup_diag, right_sides):
    length = main_diag.shape[along]
    level_total = (length - 1).bit_length()
    sub_now, main_now, sup_now, rights_now = (sub_diag, main_diag, sup_diag, tuple(right_sides))
    for level_at in range(level_total):
        stride = 1 << level_at
        sub_up = take_from(sub_now, stride, 0.0, along, True)
        main_up = take_from(main_now, stride, 1.0, along, True)
        sup_up = take_from(sup_now, stride, 0.0, along, True)
        sub_down = take_from(sub_now, stride, 0.0, along, False)
        main_down = take_from(main_now, stride, 1.0, along, False)
        sup_down = take_from(sup_now, stride, 0.0, along, False)
        factor_up = sub_now / main_up
        factor_down = sup_now / main_down
        new_main = main_now - factor_up * sup_up - factor_down * sub_down
        new_sub = -factor_up * sub_up
        new_sup = -factor_down * sup_down
        rights_now = tuple(
            (
                operand
                - factor_up * take_from(operand, stride, 0.0, along, True)
                - factor_down * take_from(operand, stride, 0.0, along, False)
                for operand in rights_now
            )
        )
        sub_now, main_now, sup_now = (new_sub, new_main, new_sup)
    return tuple((operand / main_now for operand in rights_now))


def body(history, source, diffusivity, target):
    level_count = history.shape[0]
    local_rows = diffusivity.shape[0]
    width_cells = diffusivity.shape[1]
    stiffness = float(STIFF)
    weights = memory_weights(level_count)
    memory = jnp.dot(
        weights,
        history.reshape(level_count, local_rows * width_cells),
        precision=lax.Precision.HIGHEST,
    ).reshape(local_rows, width_cells)
    driven = history[0] - memory + source
    coupling = -stiffness * diffusivity
    main_band = 1.0 + 2.0 * stiffness * diffusivity
    column_pos = lax.broadcasted_iota(jnp.int32, diffusivity.shape, 1)
    sub_x = jnp.where(column_pos == 0, 0.0, coupling)
    sup_x = jnp.where(column_pos == width_cells - 1, 0.0, coupling)
    (swept,) = cyclic_solve(1, sub_x, main_band, sup_x, (driven,))
    device_count = lax.axis_size("rows")
    total_rows = device_count * local_rows
    columns, column_diff = (
        lax.all_to_all(swept, "rows", split_axis=1, concat_axis=0, tiled=True),
        lax.all_to_all(diffusivity, "rows", split_axis=1, concat_axis=0, tiled=True),
    )
    line_pos = lax.broadcasted_iota(jnp.int32, columns.shape, 0)
    line_coupling = -stiffness * column_diff
    line_sub = jnp.where(line_pos == 0, 0.0, line_coupling)
    line_sup = jnp.where(line_pos == total_rows - 1, 0.0, line_coupling)
    (solved,) = cyclic_solve(0, line_sub, 1.0 + 2.0 * stiffness * column_diff, line_sup, (columns,))
    update = lax.all_to_all(solved, "rows", split_axis=0, concat_axis=1, tiled=True)
    mass_sum, error_sum = lax.psum((jnp.sum(update), jnp.sum((update - target) ** 2)), "rows")
    cell_count = float(total_rows * width_cells)
    return (update, jnp.stack([mass_sum / cell_count, error_sum / cell_count]))


def solution(mesh):
    in_specs = (P(None, "rows", None), P("rows", None), P("rows", None), P("rows", None))
    out_specs = (P("rows", None), P())
    return jax.shard_map(body, mesh=mesh, in_specs=in_specs, out_specs=out_specs, check_vma=False)
```

profile of v0, /device:TPU:0, one launch (start us, length us, event | category | flops | bytes accessed | tf_op | source)
XLA Modules:
  0.0 116.8 jit_solution(12748374454384149109)
XLA Ops:
  0.8 1.0 multiply_select_fusion
  2.1 12.6 %fusion = f32[1,16,4096]{2,0,1:T(1,128)S(1)} fusion(f32[1]{0:T(128)} %constant.11.clone.1, f32[31]{0:T(128)S(1)} %slice.514, f32[4,8,16,4096]{3,2,1,0:T(8,128)} %bitcast.55), kind=kOutput, calls=%fused_computation | convolution fusion | flops 25165920 | bytes 8650880 | tf_op jit(solution)/shard_map/dot_general | solution.py:67
  14.6 1.1 fusion.3
  16.0 0.3 multiply_subtract_fusion.36
  16.6 0.4 multiply_subtract_fusion.35
  17.7 0.3 multiply_subtract_fusion.33
  18.9 0.3 multiply_subtract_fusion.31
  20.0 0.3 multiply_subtract_fusion.29
  21.1 0.3 multiply_subtract_fusion.27
  22.2 0.3 multiply_subtract_fusion.25
  23.2 0.2 multiply_subtract_fusion.23
  25.1 0.8 copy_bitcast_fusion.2
  25.9 7.3 %all-to-all-start = ((f32[16,32,128]{2,0,1:T(8,128)}), f32[16,32,128]{2,0,1:T(8,128)S(1)}, u32[]{:S(2)}, u32[]{:S(2)}) async-start(f32[16,32,128]{2,0,1:T(8,128)} %copy_bitcast_fusion.2), calls=%async_computation | async-start | bytes 524288 | tf_op jit(solution)/shard_map/all_to_all | solution.py:82
  33.2 0.7 copy_bitcast_fusion.1
  33.9 9.9 %all-to-all-done = f32[16,32,128]{2,0,1:T(8,128)S(1)} async-done(((f32[16,32,128]{2,0,1:T(8,128)}), f32[16,32,128]{2,0,1:T(8,128)S(1)}, u32[]{:S(2)}, u32[]{:S(2)}) %all-to-all-start) | async-done | bytes 262176 | tf_op jit(solution)/shard_map/all_to_all | solution.py:82
  43.8 2.8 %all-to-all-start.1 = ((f32[16,32,128]{2,0,1:T(8,128)}), f32[16,32,128]{2,0,1:T(8,128)S(1)}, u32[]{:S(2)}, u32[]{:S(2)}) async-start(f32[16,32,128]{2,0,1:T(8,128)} %copy_bitcast_fusion.1), calls=%async_computation.1 | async-start | bytes 524288 | tf_op jit(solution)/shard_map/all_to_all | solution.py:83
  46.7 10.3 %all-to-all-done.1 = f32[16,32,128]{2,0,1:T(8,128)S(1)} async-done(((f32[16,32,128]{2,0,1:T(8,128)}), f32[16,32,128]{2,0,1:T(8,128)S(1)}, u32[]{:S(2)}, u32[]{:S(2)}) %all-to-all-start.1) | async-done | bytes 262176 | tf_op jit(solution)/shard_map/all_to_all | solution.py:83
  59.1 0.3 multiply_subtract_fusion.7
  59.7 0.2 multiply_subtract_fusion.5
  61.4 12.7 %all_to_all.51 = f32[32,16,128]{2,1,0:T(8,128)S(1)} all-to-all(f32[32,16,128]{2,1,0:T(8,128)S(1)} %bitcast.58), channel_id=1, replica_groups=mesh['rows'=32] {'rows'}, dimensions={0} | all-to-all | bytes 524288 | tf_op jit(solution)/shard_map/all_to_all | solution.py:90
  74.1 1.3 %multiply_reduce_fusion = (f32[]{:T(128)}, f32[16,4096]{1,0:T(8,128)}) fusion(f32[16,4096]{1,0:T(8,128)S(1)} %copy-done.2, f32[32,16,128]{2,1,0:T(8,128)S(1)} %all_to_all.51), kind=kLoop, calls=%fused_computation.10 | loop fusion | flops 196607 | bytes 786436 | tf_op jit(solution)/shard_map/reduce_sum | solution.py:91
  75.4 0.7 reduce_sum.18
  76.1 38.8 %all-reduce.164 = (f32[]{:T(128)}, f32[]{:T(128)}) all-reduce(f32[]{:T(128)} %get-tuple-element.4, f32[]{:T(128)} %reduce_sum.18), channel_id=1, replica_groups=mesh['rows'=32] {'rows'}, use_global_device_ids=true, to_apply=%region_3.4 | all-reduce | flops 2 | bytes 16 | tf_op jit(solution)/shard_map/psum | solution.py:91
  116.2 0.6 pad_maximum_fusion
  (123 shorter events, 10.2 us)
Async XLA Ops:
  0.6 15.4 %copy-start = (f32[16,4096]{1,0:T(8,128)S(1)}, f32[16,4096]{1,0:T(8,128)}, u32[]{:S(2)}) copy-start(f32[16,4096]{1,0:T(8,128)} %param.6) | copy-start | bytes 786436
  0.6 14.0 %copy-start.1 = (f32[16,4096]{1,0:T(8,128)S(1)}, f32[16,4096]{1,0:T(8,128)}, u32[]{:S(2)}) copy-start(f32[16,4096]{1,0:T(8,128)} %param.5) | copy-start | bytes 786436
  25.9 17.9 %all-to-all-start = ((f32[16,32,128]{2,0,1:T(8,128)}), f32[16,32,128]{2,0,1:T(8,128)S(1)}, u32[]{:S(2)}, u32[]{:S(2)}) async-start(f32[16,32,128]{2,0,1:T(8,128)} %copy_bitcast_fusion.2), calls=%async_computation | async-start | bytes 524288 | tf_op jit(solution)/shard_map/all_to_all | solution.py:82
  43.8 13.2 %all-to-all-start.1 = ((f32[16,32,128]{2,0,1:T(8,128)}), f32[16,32,128]{2,0,1:T(8,128)S(1)}, u32[]{:S(2)}, u32[]{:S(2)}) async-start(f32[16,32,128]{2,0,1:T(8,128)} %copy_bitcast_fusion.1), calls=%async_computation.1 | async-start | bytes 524288 | tf_op jit(solution)/shard_map/all_to_all | solution.py:83
  60.4 13.6 %copy-start.2 = (f32[16,4096]{1,0:T(8,128)S(1)}, f32[16,4096]{1,0:T(8,128)}, u32[]{:S(2)}) copy-start(f32[16,4096]{1,0:T(8,128)} %param.7) | copy-start | bytes 786436
where the time goes:
time: 117 us
  blocking collectives  51.5 us (44%)
  waiting for transfers between devices  20.2 us (17%)
  other arithmetic  13.5 us (12%)
  matrix products  12.6 us (11%)
  starting transfers between devices  10.1 us (9%)
  local copies, waits for them, and re-layouts  6.13 us (5%)
  between operations  2.82 us (2%)
    psum x1, blocking collectives, body(): lax.psum((jnp.sum(update), jnp.sum((update - target) ** 2)), 'rows')  38.8 us
    all_to_all x1, blocking collectives, body(): lax.all_to_all(solved, 'rows', split_axis=0, concat_axis=1, tiled=True)  12.7 us
    dot_general x1, matrix products, body(): jnp.dot(weights, history.reshape(level_count, local_rows * width_cells),...  12.6 us
    all_to_all x1, waiting for transfers between devices, body(): lax.all_to_all(diffusivity, 'rows', split_axis=1, concat_axis=0, tiled=True)  10.3 us
    all_to_all x1, waiting for transfers between devices, body(): lax.all_to_all(swept, 'rows', split_axis=1, concat_axis=0, tiled=True)  9.86 us
    all_to_all x1, starting transfers between devices, body(): lax.all_to_all(swept, 'rows', split_axis=1, concat_axis=0, tiled=True)  7.33 us
    sub x18, other arithmetic, cyclic_solve(): operand - factor_up * take_from(operand, stride, 0.0, along, True)  4.63 us
    all_to_all x1, starting transfers between devices, body(): lax.all_to_all(diffusivity, 'rows', split_axis=1, concat_axis=0, tiled=True)  2.8 us
  transfers between devices with their start and end apart: 2, of which 2 were waited for; matrix products, arithmetic and copies ran while one was open for 1% of the time, Pallas kernels for 0%

commit v1 on v0

v1 whole, which is shorter than its diff:
```python
import functools

import numpy as np
import jax
import jax.numpy as jnp
from jax import lax
from jax.experimental import pallas as pl
from jax.experimental.pallas import tpu as pltpu
from jax.sharding import PartitionSpec as P

STIFF = 1024
FRAC_ORDER = 0.6
LANES = 128
SUB = 8
CHUNK = 4


def driven_weights(levels):
    powered = np.arange(levels + 1, dtype=np.float64) ** (1.0 - FRAC_ORDER)
    decay = powered[1:] - powered[:-1]
    weights = np.append(decay[1:], 0.0) - np.append(0.0, decay[1:])
    combined = -weights
    combined[0] += 1.0
    return [float(w) for w in combined]


def rotate(x, shift, axis):
    size = x.shape[axis]
    shift = shift % size
    if shift == 0:
        return x
    unit = LANES if axis == 1 else SUB
    if shift % unit == 0:
        tail = lax.slice_in_dim(x, size - shift, size, axis=axis)
        head = lax.slice_in_dim(x, 0, size - shift, axis=axis)
        return jnp.concatenate([tail, head], axis)
    return pltpu.roll(x, shift, axis)


def pcr_level(lo, hi, excess, stride, axis):
    inv = 1.0 / (excess + lo + hi)
    g = lo * rotate(inv, stride, axis)
    h = hi * rotate(inv, -stride, axis)
    excess = excess + g * rotate(excess, stride, axis) + h * rotate(excess, -stride, axis)
    lo_new = g * rotate(lo, stride, axis)
    hi_new = h * rotate(hi, -stride, axis)
    return g, h, lo_new, hi_new, excess


def apply_level(d, g, h, stride, axis):
    return d + g * rotate(d, stride, axis) + h * rotate(d, -stride, axis)


def levels_of(length):
    return (length - 1).bit_length()


def kernel(nd, owners, weights, hist, src, dif, tgt, out, totals,
           hbuf, sbuf, dbuf, tbuf, acc, gx, hx, ivx, gy, hy, ivy, abuf, bbuf,
           s0, r0, s1, r1, s2, r2, xs, xr, tp, tr, gz, hz, ivz, send_sem, recv_sem, in_sem, h_sem):
    rows, width = dbuf.shape
    me = lax.axis_index("rows")
    spread = nd // owners
    nchunk = h_sem.shape[0]
    nlev_x, nlev_y, nlev_z = levels_of(width), levels_of(rows), levels_of(nd)
    stiff = float(STIFF)
    mine = me // spread

    load_dif = pltpu.make_async_copy(dif, dbuf, in_sem.at[0])
    load_dif.start()
    loads = []
    for c in range(nchunk):
        part = pl.ds(c * CHUNK, CHUNK)
        copy = pltpu.make_async_copy(hist.at[part], hbuf.at[part], h_sem.at[c])
        copy.start()
        loads.append(copy)
    load_src = pltpu.make_async_copy(src, sbuf, in_sem.at[1])
    load_src.start()
    load_tgt = pltpu.make_async_copy(tgt, tbuf, in_sem.at[2])
    load_tgt.start()

    barrier = pltpu.get_barrier_semaphore()

    @pl.loop(1, nd)
    def _(k):
        pl.semaphore_signal(barrier, inc=1, device_id=(lax.rem(me + k, nd),),
                            device_id_type=pl.DeviceIdType.MESH)

    def lane_part(o):
        return pl.ds(pl.multiple_of(o * LANES, LANES), LANES)

    is_owner = lax.rem(me, spread) == 0

    def when_owner(fn):
        if spread == 1:
            fn()
        else:
            pl.when(is_owner)(fn)

    def remote(src_ref, dst_ref, phase, dev):
        return pltpu.make_async_remote_copy(
            src_ref=src_ref, dst_ref=dst_ref, send_sem=send_sem.at[phase], recv_sem=recv_sem.at[phase],
            device_id=(dev,), device_id_type=pl.DeviceIdType.MESH)

    def scatter(s_ref, r_ref, phase):
        if spread == 1:
            @pl.loop(1, nd)
            def _(k):
                o = lax.rem(me + k, nd)
                remote(s_ref.at[:, lane_part(o)], r_ref.at[me], phase, o).start()
            r_ref[me] = s_ref[:, lane_part(me)]
        else:
            @pl.loop(0, owners)
            def _(o):
                @pl.when(o * spread != me)
                def _():
                    remote(s_ref.at[:, lane_part(o)], r_ref.at[me], phase, o * spread).start()

            @pl.when(is_owner)
            def _():
                r_ref[me] = s_ref[:, lane_part(mine)]

    def wait_all(ref, sem):
        pltpu.make_async_copy(ref, ref, sem).wait()

    def wait_gathered(r_ref, phase):
        wait_all(r_ref.at[pl.ds(0, nd - 1)], recv_sem.at[phase])

    def wait_from_owners(ref_of, phase):
        if spread == 1:
            wait_all(ref_of(owners - 1), recv_sem.at[phase])
        else:
            @pl.when(is_owner)
            def _():
                wait_all(ref_of(owners - 1), recv_sem.at[phase])

            @pl.when(jnp.logical_not(is_owner))
            def _():
                wait_all(ref_of(owners), recv_sem.at[phase])

    load_dif.wait()

    last = rows - 1
    pieces = 4
    piece = width // pieces

    def column_prep(i, carry):
        lanes = pl.ds(pl.multiple_of(i * piece, LANES), piece)
        inv_c = 1.0 / (stiff * dbuf[:, lanes])
        pos = lax.broadcasted_iota(jnp.int32, inv_c.shape, 0)
        is_last = pos == last
        zero, one = jnp.zeros_like(inv_c), jnp.ones_like(inv_c)
        lo = jnp.where((pos == 0) | is_last, zero, one)
        hi = jnp.where(pos >= last - 1, zero, one)
        excess = jnp.where(is_last, one, 2.0 + inv_c - lo - hi)
        inner = (pos > 0) & (pos < last - 1)
        excess = jnp.where(inner, inv_c, excess)
        a = jnp.where(pos == 0, one, zero)
        b = jnp.where(pos >= last - 1, one, zero)
        for k in range(nlev_y):
            g, h, lo, hi, excess = pcr_level(lo, hi, excess, 1 << k, 0)
            gy[k, :, lanes] = g
            hy[k, :, lanes] = h
            a = apply_level(a, g, h, 1 << k, 0)
            b = apply_level(b, g, h, 1 << k, 0)
        inv = 1.0 / (excess + lo + hi)
        ivy[:, lanes] = inv
        a, b = a * inv, b * inv
        abuf[:, lanes] = a
        bbuf[:, lanes] = b
        s0[0:1, lanes] = 2.0 + inv_c[last:last + 1] - b[last - 1:last]
        s0[1:2, lanes] = a[0:1]
        s0[2:3, lanes] = a[last - 1:last]
        s0[3:4, lanes] = jnp.sum(a * a, 0, keepdims=True)
        s0[4:5, lanes] = jnp.sum(a * b, 0, keepdims=True)
        s0[5:6, lanes] = jnp.sum(b * b, 0, keepdims=True)
        s0[6:7, lanes] = jnp.sum(a, 0, keepdims=True)
        s0[7:8, lanes] = jnp.sum(b, 0, keepdims=True)
        return carry

    lax.fori_loop(0, pieces, column_prep, 0)

    pl.semaphore_wait(barrier, nd - 1)
    scatter(s0, r0, 0)

    def row_prep(i, carry):
        part = pl.ds(pl.multiple_of(i * SUB, SUB), SUB)
        inv_c = 1.0 / (stiff * dbuf[part, :])
        pos = lax.broadcasted_iota(jnp.int32, inv_c.shape, 1)
        zero, one = jnp.zeros_like(inv_c), jnp.ones_like(inv_c)
        lo = jnp.where(pos == 0, zero, one)
        hi = jnp.where(pos == width - 1, zero, one)
        excess = jnp.where((pos == 0) | (pos == width - 1), inv_c + 1.0, inv_c)
        for k in range(nlev_x):
            g, h, lo, hi, excess = pcr_level(lo, hi, excess, 1 << k, 1)
            gx[k, part, :] = g
            hx[k, part, :] = h
        ivx[part, :] = 1.0 / (excess + lo + hi)
        return carry

    lax.fori_loop(0, rows // SUB, row_prep, 0)

    load_src.wait()
    for c in range(nchunk):
        loads[c].wait()
        base = sbuf if c == 0 else acc
        total = base[...]
        for k in range(c * CHUNK, (c + 1) * CHUNK):
            total = total + weights[k] * hbuf[k]
        acc[...] = total

    def row_solve(i, carry):
        part = pl.ds(pl.multiple_of(i * SUB, SUB), SUB)
        inv_c = 1.0 / (stiff * dbuf[part, :])
        d = acc[part, :] * inv_c
        for k in range(nlev_x):
            d = apply_level(d, gx[k, part, :], hx[k, part, :], 1 << k, 1)
        acc[part, :] = d * ivx[part, :] * inv_c
        return carry

    lax.fori_loop(0, rows // SUB, row_solve, 0)

    def column_solve(i, carry):
        lanes = pl.ds(pl.multiple_of(i * piece, LANES), piece)
        full = acc[:, lanes]
        pos = lax.broadcasted_iota(jnp.int32, full.shape, 0)
        d = jnp.where(pos == last, 0.0, full)
        for k in range(nlev_y):
            d = apply_level(d, gy[k, :, lanes], hy[k, :, lanes], 1 << k, 0)
        d = d * ivy[:, lanes]
        s1[0:1, lanes] = full[last:last + 1] + d[last - 1:last]
        s1[1:2, lanes] = d[0:1]
        acc[:, lanes] = d
        return carry

    lax.fori_loop(0, pieces, column_solve, 0)
    scatter(s1, r1, 1)

    load_tgt.wait()

    def error_parts(i, carry):
        lanes = pl.ds(pl.multiple_of(i * piece, LANES), piece)
        u = acc[:, lanes]
        gap = u - tbuf[:, lanes]
        s2[0:1, lanes] = jnp.sum(gap * abuf[:, lanes], 0, keepdims=True)
        s2[1:2, lanes] = jnp.sum(gap * bbuf[:, lanes], 0, keepdims=True)
        s2[2:3, lanes] = jnp.sum(gap * gap, 0, keepdims=True)
        s2[3:4, lanes] = jnp.sum(u, 0, keepdims=True)
        return carry

    lax.fori_loop(0, pieces, error_parts, 0)
    scatter(s2, r2, 2)

    def owner_work():
        wait_gathered(r0, 0)
        block = lax.broadcasted_iota(jnp.int32, (nd, LANES), 0)
        at_end = block == nd - 1

        def next_block(x):
            return jnp.where(at_end, 0.0, rotate(x, -1, 0))

        lo = jnp.where(block == 0, 0.0, r0[:, 2, :])
        hi = next_block(lo)
        excess = r0[:, 0, :] - next_block(r0[:, 1, :]) - lo - hi
        for k in range(nlev_z):
            g, h, lo, hi, excess = pcr_level(lo, hi, excess, 1 << k, 0)
            gz[k] = g
            hz[k] = h
        ivz[...] = 1.0 / (excess + lo + hi)
        wait_gathered(r1, 1)
        x = r1[:, 0, :] + next_block(r1[:, 1, :])
        for k in range(nlev_z):
            x = apply_level(x, gz[k], hz[k], 1 << k, 0)
        x = x * ivz[...]
        before = jnp.where(block == 0, 0.0, rotate(x, 1, 0))
        xs[:, 0, :] = before
        xs[:, 1, :] = x

        @pl.loop(1, nd)
        def _(k):
            dev = lax.rem(me + k, nd)
            remote(xs.at[dev], xr.at[:, lane_part(mine)], 3, dev).start()
        xr[:, lane_part(mine)] = xs[me]

        wait_gathered(r2, 2)
        mass = r2[:, 3, :] + r0[:, 6, :] * before + r0[:, 7, :] * x
        err = (r2[:, 2, :] + before * (2.0 * r2[:, 0, :] + r0[:, 3, :] * before + 2.0 * r0[:, 4, :] * x)
               + x * (2.0 * r2[:, 1, :] + r0[:, 5, :] * x))
        tp[0:1, :] = jnp.sum(mass, 0, keepdims=True)
        tp[1:2, :] = jnp.sum(err, 0, keepdims=True)

        @pl.loop(1, nd)
        def _(k):
            dev = lax.rem(me + k, nd)
            remote(tp, tr.at[mine], 4, dev).start()
        tr[mine] = tp[...]

    when_owner(owner_work)

    wait_from_owners(lambda n: xr.at[:, pl.ds(0, n * LANES)], 3)

    def finish(i, carry):
        lanes = pl.ds(pl.multiple_of(i * piece, LANES), piece)
        out[:, lanes] = (acc[:, lanes] + abuf[:, lanes] * xr[0:1, lanes] + bbuf[:, lanes] * xr[1:2, lanes])
        return carry

    lax.fori_loop(0, pieces, finish, 0)

    wait_from_owners(lambda n: tr.at[pl.ds(0, n)], 4)
    scale = 1.0 / float(nd * rows * width)
    totals[0] = jnp.sum(tr[:, 0, :]) * scale
    totals[1] = jnp.sum(tr[:, 1, :]) * scale

    def wait_sent(ref_of, phase):
        if spread == 1:
            wait_all(ref_of(owners - 1), send_sem.at[phase])
        else:
            @pl.when(is_owner)
            def _():
                wait_all(ref_of(owners - 1), send_sem.at[phase])

            @pl.when(jnp.logical_not(is_owner))
            def _():
                wait_all(ref_of(owners), send_sem.at[phase])

    for phase, ref in enumerate((s0, s1, s2)):
        wait_sent(lambda n, ref=ref: ref.at[:, pl.ds(0, n * LANES)], phase)

    def owner_sent():
        wait_all(xs.at[pl.ds(0, nd - 1)], send_sem.at[3])
        wait_all(xs.at[pl.ds(0, nd - 1)], send_sem.at[4])

    when_owner(owner_sent)


def solution(mesh):
    nd = mesh.shape["rows"]

    def body(history, source, diffusivity, target):
        levels, rows, width = history.shape
        owners = min(nd, width // LANES)
        f32 = jnp.float32
        vm = pltpu.VMEM
        nx, ny, nz = levels_of(width), levels_of(rows), levels_of(nd)
        field = vm((rows, width), f32)
        return pl.pallas_call(
            functools.partial(kernel, nd, owners, driven_weights(levels)),
            out_shape=(jax.ShapeDtypeStruct((rows, width), f32), jax.ShapeDtypeStruct((2,), f32)),
            in_specs=[pl.BlockSpec(memory_space=pl.ANY)] * 4,
            out_specs=(pl.BlockSpec(memory_space=pltpu.VMEM), pl.BlockSpec(memory_space=pltpu.SMEM)),
            scratch_shapes=[
                vm((levels, rows, width), f32), field, field, field, field,
                vm((nx, rows, width), f32), vm((nx, rows, width), f32), field,
                vm((ny, rows, width), f32), vm((ny, rows, width), f32), field, field, field,
                vm((8, width), f32), vm((nd, 8, LANES), f32),
                vm((2, width), f32), vm((nd, 2, LANES), f32),
                vm((4, width), f32), vm((nd, 4, LANES), f32),
                vm((nd, 2, LANES), f32), vm((2, width), f32),
                vm((2, LANES), f32), vm((owners, 2, LANES), f32),
                vm((nz, nd, LANES), f32), vm((nz, nd, LANES), f32), vm((nd, LANES), f32),
                pltpu.SemaphoreType.DMA((5,)), pltpu.SemaphoreType.DMA((5,)),
                pltpu.SemaphoreType.DMA((3,)), pltpu.SemaphoreType.DMA((levels // CHUNK,)),
            ],
            compiler_params=pltpu.CompilerParams(collective_id=0, has_side_effects=True),
        )(history, source, diffusivity, target)

    in_specs = (P(None, "rows", None), P("rows", None), P("rows", None), P("rows", None))
    return jax.shard_map(body, mesh=mesh, in_specs=in_specs, out_specs=(P("rows", None), P()), check_vma=False)
```

time: 117 us -> 28.7 us (0.25)
  blocking collectives: 51.5 us -> 0 us
  Pallas kernels: 0 us -> 25.1 us
  waiting for transfers between devices: 20.2 us -> 0 us
  other arithmetic: 13.5 us -> 0 us
  matrix products: 12.6 us -> 0 us
  starting transfers between devices: 10.1 us -> 0 us
  local copies, waits for them, and re-layouts: 6.13 us -> 2.8 us
  between operations: 2.82 us -> 0.64 us
    psum x1 -> x0, blocking collectives: 38.8 us -> none  [body(): lax.psum((jnp.sum(update), jnp.sum((update - target) ** 2)), 'rows')]
    pallas_call x0 -> x1, Pallas kernels: none -> 25.1 us  [body(): pl.pallas_call(functools.partial(kernel, nd, owners, driven_weights(level...]
    all_to_all x2 -> x0, waiting for transfers between devices: 20.2 us -> none  [the longest x1 10.3 us: body(): lax.all_to_all(diffusivity, 'rows', split_axis=1, concat_axis=0, tiled=True)]
    all_to_all x1 -> x0, blocking collectives: 12.7 us -> none  [body(): lax.all_to_all(solved, 'rows', split_axis=0, concat_axis=1, tiled=True)]
    dot_general x1 -> x0, matrix products: 12.6 us -> none  [body(): jnp.dot(weights, history.reshape(level_count, local_rows * width_cells),...]
    all_to_all x2 -> x0, starting transfers between devices: 10.1 us -> none  [the longest x1 7.33 us: body(): lax.all_to_all(swept, 'rows', split_axis=1, concat_axis=0, tiled=True)]
    sub x36 -> x0, other arithmetic: 7.43 us -> none  [the longest x18 4.63 us: cyclic_solve(): operand - factor_up * take_from(operand, stride, 0.0, along, True)]
    slice x83 -> x0, local copies, waits for them, and re-layouts: 5.39 us -> none  [the longest x41 2.68 us: take_from(): kept = lax.slice_in_dim(array_in, stride, length, 1, along)]
  transfers between devices with their start and end apart: 2 -> 0, of which waited for: 2 -> 0; matrix products, arithmetic and copies ran while one was open for 1% -> 0% of each run, Pallas kernels for 0% -> 0%
where the time goes in v1:
time: 28.7 us; the launch traced here: 28.5 us
  Pallas kernels  25.1 us (87%)
  local copies, waits for them, and re-layouts  2.8 us (10%)
  between operations  0.64 us (2%)
    pallas_call x1, Pallas kernels, body(): pl.pallas_call(functools.partial(kernel, nd, owners, driven_weights(level...  25.1 us
    unnamed x2, local copies, waits for them, and re-layouts  2.8 us

profile of v1, /device:TPU:0, one launch (start us, length us, event | category | flops | bytes accessed | tf_op | source)
XLA Modules:
  0.0 28.5 jit_solution(15660933075195110511)
XLA Ops:
  0.6 25.1 %shard_map.59 = (f32[16,4096]{1,0:T(8,128)}, f32[2]{0:T(128)}) custom-call(f32[32,16,4096]{2,1,0:T(8,128)} %hist.1, f32[16,4096]{1,0:T(8,128)} %src.1, f32[16,4096]{1,0:T(8,128)} %dif.1, f32[16,4096]{1,0:T(8,128)} %tgt.1), custom_call_target="tpu_custom_call" | custom-call | tf_op jit(solution)/shard_map/pallas_call | solution.py:346
  25.7 1.7 %copy.8 = f32[16,4096]{1,0:T(8,128)} copy(f32[16,4096]{1,0:T(8,128)} %get-tuple-element.4) | data formatting | bytes 524288
  27.4 1.1 %copy.9 = f32[2]{0:T(128)} copy(f32[2]{0:T(128)} %get-tuple-element.5) | data formatting | bytes 16

commit v2 on v1

--- a/solution.py
+++ b/solution.py
@@ -55,16 +55,17 @@
     return (length - 1).bit_length()
 
 
-def kernel(nd, owners, weights, hist, src, dif, tgt, out, totals,
+def kernel(nd, first, owners, spread, weights, hist, src, dif, tgt, free_out, a_out, b_out, xr, tr,
            hbuf, sbuf, dbuf, tbuf, acc, gx, hx, ivx, gy, hy, ivy, abuf, bbuf,
-           s0, r0, s1, r1, s2, r2, xs, xr, tp, tr, gz, hz, ivz, send_sem, recv_sem, in_sem, h_sem):
+           s0, r0, s1, r1, s2, r2, xs, tp, gz, hz, ivz, send_sem, recv_sem, in_sem, h_sem):
     rows, width = dbuf.shape
     me = lax.axis_index("rows")
-    spread = nd // owners
+    cols = width // owners
     nchunk = h_sem.shape[0]
     nlev_x, nlev_y, nlev_z = levels_of(width), levels_of(rows), levels_of(nd)
     stiff = float(STIFF)
-    mine = me // spread
+    mine = (me - first) // spread
+    is_owner = (me >= first) & (me < first + owners * spread) & (lax.rem(me - first + nd, spread) == 0)
 
     load_dif = pltpu.make_async_copy(dif, dbuf, in_sem.at[0])
     load_dif.start()
@@ -81,21 +82,31 @@
 
     barrier = pltpu.get_barrier_semaphore()
 
-    @pl.loop(1, nd)
-    def _(k):
-        pl.semaphore_signal(barrier, inc=1, device_id=(lax.rem(me + k, nd),),
-                            device_id_type=pl.DeviceIdType.MESH)
+    def greet(dev):
+        pl.semaphore_signal(barrier, inc=1, device_id=(dev,), device_id_type=pl.DeviceIdType.MESH)
+
+    def to_others(fn):
+        @pl.loop(1, nd)
+        def _(k):
+            fn(lax.rem(me + k, nd))
+
+    def to_owners(fn):
+        @pl.loop(0, owners)
+        def _(o):
+            dev = first + o * spread
+
+            @pl.when(dev != me)
+            def _():
+                fn(dev, o)
+
+    def by_role(owner_fn, other_fn):
+        pl.when(is_owner)(owner_fn)
+        pl.when(jnp.logical_not(is_owner))(other_fn)
+
+    by_role(lambda: to_others(greet), lambda: to_owners(lambda dev, o: greet(dev)))
 
     def lane_part(o):
-        return pl.ds(pl.multiple_of(o * LANES, LANES), LANES)
-
-    is_owner = lax.rem(me, spread) == 0
-
-    def when_owner(fn):
-        if spread == 1:
-            fn()
-        else:
-            pl.when(is_owner)(fn)
+        return pl.ds(pl.multiple_of(o * cols, LANES), cols)
 
     def remote(src_ref, dst_ref, phase, dev):
         return pltpu.make_async_remote_copy(
@@ -103,22 +114,11 @@
             device_id=(dev,), device_id_type=pl.DeviceIdType.MESH)
 
     def scatter(s_ref, r_ref, phase):
-        if spread == 1:
-            @pl.loop(1, nd)
-            def _(k):
-                o = lax.rem(me + k, nd)
-                remote(s_ref.at[:, lane_part(o)], r_ref.at[me], phase, o).start()
-            r_ref[me] = s_ref[:, lane_part(me)]
-        else:
-            @pl.loop(0, owners)
-            def _(o):
-                @pl.when(o * spread != me)
-                def _():
-                    remote(s_ref.at[:, lane_part(o)], r_ref.at[me], phase, o * spread).start()
-
-            @pl.when(is_owner)
-            def _():
-                r_ref[me] = s_ref[:, lane_part(mine)]
+        to_owners(lambda dev, o: remote(s_ref.at[:, lane_part(o)], r_ref.at[me], phase, dev).start())
+
+        @pl.when(is_owner)
+        def _():
+            r_ref[me] = s_ref[:, lane_part(mine)]
 
     def wait_all(ref, sem):
         pltpu.make_async_copy(ref, ref, sem).wait()
@@ -126,17 +126,8 @@
     def wait_gathered(r_ref, phase):
         wait_all(r_ref.at[pl.ds(0, nd - 1)], recv_sem.at[phase])
 
-    def wait_from_owners(ref_of, phase):
-        if spread == 1:
-            wait_all(ref_of(owners - 1), recv_sem.at[phase])
-        else:
-            @pl.when(is_owner)
-            def _():
-                wait_all(ref_of(owners - 1), recv_sem.at[phase])
-
-            @pl.when(jnp.logical_not(is_owner))
-            def _():
-                wait_all(ref_of(owners), recv_sem.at[phase])
+    def wait_from_owners(ref_of, sem):
+        by_role(lambda: wait_all(ref_of(owners - 1), sem), lambda: wait_all(ref_of(owners), sem))
 
     load_dif.wait()
 
@@ -180,8 +171,10 @@
 
     lax.fori_loop(0, pieces, column_prep, 0)
 
-    pl.semaphore_wait(barrier, nd - 1)
-    scatter(s0, r0, 0)
+    put_a = pltpu.make_async_copy(abuf, a_out, in_sem.at[3])
+    put_b = pltpu.make_async_copy(bbuf, b_out, in_sem.at[4])
+    put_a.start()
+    put_b.start()
 
     def row_prep(i, carry):
         part = pl.ds(pl.multiple_of(i * SUB, SUB), SUB)
@@ -200,6 +193,9 @@
 
     lax.fori_loop(0, rows // SUB, row_prep, 0)
 
+    by_role(lambda: pl.semaphore_wait(barrier, nd - 1), lambda: pl.semaphore_wait(barrier, owners))
+    scatter(s0, r0, 0)
+
     load_src.wait()
     for c in range(nchunk):
         loads[c].wait()
@@ -235,6 +231,8 @@
 
     lax.fori_loop(0, pieces, column_solve, 0)
     scatter(s1, r1, 1)
+    put_free = pltpu.make_async_copy(acc, free_out, in_sem.at[5])
+    put_free.start()
 
     load_tgt.wait()
 
@@ -253,7 +251,7 @@
 
     def owner_work():
         wait_gathered(r0, 0)
-        block = lax.broadcasted_iota(jnp.int32, (nd, LANES), 0)
+        block = lax.broadcasted_iota(jnp.int32, (nd, cols), 0)
         at_end = block == nd - 1
 
         def next_block(x):
@@ -276,10 +274,7 @@
         xs[:, 0, :] = before
         xs[:, 1, :] = x
 
-        @pl.loop(1, nd)
-        def _(k):
-            dev = lax.rem(me + k, nd)
-            remote(xs.at[dev], xr.at[:, lane_part(mine)], 3, dev).start()
+        to_others(lambda dev: remote(xs.at[dev], xr.at[:, lane_part(mine)], 3, dev).start())
         xr[:, lane_part(mine)] = xs[me]
 
         wait_gathered(r2, 2)
@@ -289,80 +284,72 @@
         tp[0:1, :] = jnp.sum(mass, 0, keepdims=True)
         tp[1:2, :] = jnp.sum(err, 0, keepdims=True)
 
-        @pl.loop(1, nd)
-        def _(k):
-            dev = lax.rem(me + k, nd)
-            remote(tp, tr.at[mine], 4, dev).start()
+        to_others(lambda dev: remote(tp, tr.at[mine], 4, dev).start())
         tr[mine] = tp[...]
 
-    when_owner(owner_work)
-
-    wait_from_owners(lambda n: xr.at[:, pl.ds(0, n * LANES)], 3)
-
-    def finish(i, carry):
-        lanes = pl.ds(pl.multiple_of(i * piece, LANES), piece)
-        out[:, lanes] = (acc[:, lanes] + abuf[:, lanes] * xr[0:1, lanes] + bbuf[:, lanes] * xr[1:2, lanes])
-        return carry
-
-    lax.fori_loop(0, pieces, finish, 0)
-
-    wait_from_owners(lambda n: tr.at[pl.ds(0, n)], 4)
-    scale = 1.0 / float(nd * rows * width)
+    pl.when(is_owner)(owner_work)
+
+    put_a.wait()
+    put_b.wait()
+    put_free.wait()
+    for phase, ref in enumerate((s0, s1, s2)):
+        wait_from_owners(lambda n, ref=ref: ref.at[:, pl.ds(0, n * cols)], send_sem.at[phase])
+    wait_from_owners(lambda n: xr.at[:, pl.ds(0, n * cols)], recv_sem.at[3])
+    wait_from_owners(lambda n: tr.at[pl.ds(0, n)], recv_sem.at[4])
+
+    @pl.when(is_owner)
+    def _():
+        wait_all(xs.at[pl.ds(0, nd - 1)], send_sem.at[3])
+        wait_all(xs.at[pl.ds(0, nd - 1)], send_sem.at[4])
+
+
+def finish(cells, free, a, b, xr, tr, out, totals):
+    out[...] = free[...] + a[...] * xr[0:1, :] + b[...] * xr[1:2, :]
+    scale = 1.0 / float(cells)
     totals[0] = jnp.sum(tr[:, 0, :]) * scale
     totals[1] = jnp.sum(tr[:, 1, :]) * scale
 
-    def wait_sent(ref_of, phase):
-        if spread == 1:
-            wait_all(ref_of(owners - 1), send_sem.at[phase])
-        else:
-            @pl.when(is_owner)
-            def _():
-                wait_all(ref_of(owners - 1), send_sem.at[phase])
-
-            @pl.when(jnp.logical_not(is_owner))
-            def _():
-                wait_all(ref_of(owners), send_sem.at[phase])
-
-    for phase, ref in enumerate((s0, s1, s2)):
-        wait_sent(lambda n, ref=ref: ref.at[:, pl.ds(0, n * LANES)], phase)
-
-    def owner_sent():
-        wait_all(xs.at[pl.ds(0, nd - 1)], send_sem.at[3])
-        wait_all(xs.at[pl.ds(0, nd - 1)], send_sem.at[4])
-
-    when_owner(owner_sent)
-
 
 def solution(mesh):
     nd = mesh.shape["rows"]
 
     def body(history, source, diffusivity, target):
         levels, rows, width = history.shape
-        owners = min(nd, width // LANES)
+        middle = max(nd // 2, 1)
+        owners = min(middle, width // LANES)
+        first, spread, cols = nd // 4, middle // owners, width // owners
         f32 = jnp.float32
         vm = pltpu.VMEM
         nx, ny, nz = levels_of(width), levels_of(rows), levels_of(nd)
         field = vm((rows, width), f32)
-        return pl.pallas_call(
-            functools.partial(kernel, nd, owners, driven_weights(levels)),
-            out_shape=(jax.ShapeDtypeStruct((rows, width), f32), jax.ShapeDtypeStruct((2,), f32)),
-            in_specs=[pl.BlockSpec(memory_space=pl.ANY)] * 4,
-            out_specs=(pl.BlockSpec(memory_space=pltpu.VMEM), pl.BlockSpec(memory_space=pltpu.SMEM)),
+        whole = jax.ShapeDtypeStruct((rows, width), f32)
+        in_hbm, in_vmem = pl.BlockSpec(memory_space=pl.ANY), pl.BlockSpec(memory_space=pltpu.VMEM)
+        parts = pl.pallas_call(
+            functools.partial(kernel, nd, first, owners, spread, driven_weights(levels)),
+            out_shape=(whole, whole, whole, jax.ShapeDtypeStruct((2, width), f32),
+                       jax.ShapeDtypeStruct((owners, 2, cols), f32)),
+            in_specs=[in_hbm] * 4,
+            out_specs=(in_hbm, in_hbm, in_hbm, in_vmem, in_vmem),
             scratch_shapes=[
                 vm((levels, rows, width), f32), field, field, field, field,
                 vm((nx, rows, width), f32), vm((nx, rows, width), f32), field,
                 vm((ny, rows, width), f32), vm((ny, rows, width), f32), field, field, field,
-                vm((8, width), f32), vm((nd, 8, LANES), f32),
-                vm((2, width), f32), vm((nd, 2, LANES), f32),
-                vm((4, width), f32), vm((nd, 4, LANES), f32),
-                vm((nd, 2, LANES), f32), vm((2, width), f32),
-                vm((2, LANES), f32), vm((owners, 2, LANES), f32),
-                vm((nz, nd, LANES), f32), vm((nz, nd, LANES), f32), vm((nd, LANES), f32),
+                vm((8, width), f32), vm((nd, 8, cols), f32),
+                vm((2, width), f32), vm((nd, 2, cols), f32),
+                vm((4, width), f32), vm((nd, 4, cols), f32),
+                vm((nd, 2, cols), f32), vm((2, cols), f32),
+                vm((nz, nd, cols), f32), vm((nz, nd, cols), f32), vm((nd, cols), f32),
                 pltpu.SemaphoreType.DMA((5,)), pltpu.SemaphoreType.DMA((5,)),
-                pltpu.SemaphoreType.DMA((3,)), pltpu.SemaphoreType.DMA((levels // CHUNK,)),
+                pltpu.SemaphoreType.DMA((6,)), pltpu.SemaphoreType.DMA((levels // CHUNK,)),
             ],
             compiler_params=pltpu.CompilerParams(collective_id=0, has_side_effects=True),
         )(history, source, diffusivity, target)
+        return pl.pallas_call(
+            functools.partial(finish, nd * rows * width),
+            out_shape=(whole, jax.ShapeDtypeStruct((2,), f32)),
+            in_specs=[in_vmem] * 5,
+            out_specs=(in_vmem, pl.BlockSpec(memory_space=pltpu.SMEM)),
+        )(*parts)
 
     in_specs = (P(None, "rows", None), P("rows", None), P("rows", None), P("rows", None))
     return jax.shard_map(body, mesh=mesh, in_specs=in_specs, out_specs=(P("rows", None), P()), check_vma=False)

time: 28.7 us -> 26.6 us (0.927)
  local copies, waits for them, and re-layouts: 2.8 us -> 0 us
  Pallas kernels: 25.1 us -> 25.8 us
    unnamed x2 -> x0, local copies, waits for them, and re-layouts: 2.8 us -> none
    pallas_call x1 -> x2, Pallas kernels: 25.1 us -> 25.8 us  [the longest x1 23.9 us: body(): pl.pallas_call(functools.partial(kernel, nd, first, owners, spread, drive...]
where the time goes in v2:
time: 26.6 us; the launch traced here: 26.5 us
  Pallas kernels  25.8 us (97%)
  between operations  0.64 us (2%)
    pallas_call x1, Pallas kernels, body(): pl.pallas_call(functools.partial(kernel, nd, first, owners, spread, drive...  23.9 us
    pallas_call x1, Pallas kernels, body(): pl.pallas_call(functools.partial(finish, nd * rows * width), out_shape=(w...  1.93 us

profile of v2, /device:TPU:0, one launch (start us, length us, event | category | flops | bytes accessed | tf_op | source)
XLA Modules:
  0.0 26.5 jit_solution(12075565551359183944)
XLA Ops:
  0.6 23.9 %shard_map.59 = (f32[16,4096]{1,0:T(8,128)}, f32[16,4096]{1,0:T(8,128)}, f32[16,4096]{1,0:T(8,128)}, f32[2,4096]{1,0:T(2,128)}, f32[16,2,256]{2,1,0:T(2,128)}) custom-call(f32[32,16,4096]{2,1,0:T(8,128)} %hist.1, f32[16,4096]{1,0:T(8,128)} %src.1, f32[16,4096]{1,0:T(8,128)} %dif.1, f32[16,4096]{1,0:T(8,128)} %tgt.1), custom_call_target="tpu_custom_call" | custom-call | tf_op jit(solution)/shard_map/pallas_call | solution.py:327
  24.5 1.9 %shard_map.60 = (f32[16,4096]{1,0:T(8,128)}, f32[2]{0:T(128)}) custom-call(f32[16,4096]{1,0:T(8,128)} %get-tuple-element.7.free, f32[16,4096]{1,0:T(8,128)} %get-tuple-element.8.a, f32[16,4096]{1,0:T(8,128)} %get-tuple-element.9.b, f32[2,4096]{1,0:T(2,128)} %get-tuple-element.10.xr, f32[16,2,256]{2,1,0:T(2,128)} %get-tuple-element.11.tr), custom_call_target="tpu_custom_call" | custom-call | tf_op jit(solution)/shard_map/pallas_call | solution.py:347

commit v3 on v2

--- a/solution.py
+++ b/solution.py
@@ -12,7 +12,8 @@
 FRAC_ORDER = 0.6
 LANES = 128
 SUB = 8
-CHUNK = 4
+CHUNK = 8
+SUMMED = 4
 
 
 def driven_weights(levels):
@@ -37,6 +38,10 @@
     return pltpu.roll(x, shift, axis)
 
 
+def reciprocal(x):
+    return 1.0 / x
+
+
 def pcr_level(lo, hi, excess, stride, axis):
     inv = 1.0 / (excess + lo + hi)
     g = lo * rotate(inv, stride, axis)
@@ -45,6 +50,14 @@
     lo_new = g * rotate(lo, stride, axis)
     hi_new = h * rotate(hi, -stride, axis)
     return g, h, lo_new, hi_new, excess
+
+
+def pcr_main_level(lo, hi, main, stride, axis):
+    inv = reciprocal(main)
+    g = lo * rotate(inv, stride, axis)
+    h = hi * rotate(inv, -stride, axis)
+    main = main - g * lo - h * hi
+    return g, h, g * rotate(lo, stride, axis), h * rotate(hi, -stride, axis), main
 
 
 def apply_level(d, g, h, stride, axis):
@@ -92,7 +105,8 @@
 
     def to_owners(fn):
         @pl.loop(0, owners)
-        def _(o):
+        def _(k):
+            o = lax.rem(k + me, owners)
             dev = first + o * spread
 
             @pl.when(dev != me)
@@ -176,38 +190,49 @@
     put_a.start()
     put_b.start()
 
+    by_role(lambda: pl.semaphore_wait(barrier, nd - 1), lambda: pl.semaphore_wait(barrier, owners))
+    scatter(s0, r0, 0)
+
     def row_prep(i, carry):
         part = pl.ds(pl.multiple_of(i * SUB, SUB), SUB)
         inv_c = 1.0 / (stiff * dbuf[part, :])
+        dbuf[part, :] = inv_c
         pos = lax.broadcasted_iota(jnp.int32, inv_c.shape, 1)
         zero, one = jnp.zeros_like(inv_c), jnp.ones_like(inv_c)
         lo = jnp.where(pos == 0, zero, one)
         hi = jnp.where(pos == width - 1, zero, one)
         excess = jnp.where((pos == 0) | (pos == width - 1), inv_c + 1.0, inv_c)
         for k in range(nlev_x):
-            g, h, lo, hi, excess = pcr_level(lo, hi, excess, 1 << k, 1)
+            if k < SUMMED:
+                g, h, lo, hi, excess = pcr_level(lo, hi, excess, 1 << k, 1)
+                main = excess + lo + hi
+            else:
+                g, h, lo, hi, main = pcr_main_level(lo, hi, main, 1 << k, 1)
             gx[k, part, :] = g
             hx[k, part, :] = h
-        ivx[part, :] = 1.0 / (excess + lo + hi)
+        ivx[part, :] = reciprocal(main)
         return carry
 
     lax.fori_loop(0, rows // SUB, row_prep, 0)
-
-    by_role(lambda: pl.semaphore_wait(barrier, nd - 1), lambda: pl.semaphore_wait(barrier, owners))
-    scatter(s0, r0, 0)
 
     load_src.wait()
     for c in range(nchunk):
         loads[c].wait()
         base = sbuf if c == 0 else acc
-        total = base[...]
-        for k in range(c * CHUNK, (c + 1) * CHUNK):
-            total = total + weights[k] * hbuf[k]
-        acc[...] = total
+
+        def accumulate(i, carry):
+            lanes = pl.ds(pl.multiple_of(i * piece, LANES), piece)
+            total = base[:, lanes]
+            for k in range(c * CHUNK, (c + 1) * CHUNK):
+                total = total + weights[k] * hbuf[k, :, lanes]
+            acc[:, lanes] = total
+            return carry
+
+        lax.fori_loop(0, pieces, accumulate, 0)
 
     def row_solve(i, carry):
         part = pl.ds(pl.multiple_of(i * SUB, SUB), SUB)
-        inv_c = 1.0 / (stiff * dbuf[part, :])
+        inv_c = dbuf[part, :]
         d = acc[part, :] * inv_c
         for k in range(nlev_x):
             d = apply_level(d, gx[k, part, :], hx[k, part, :], 1 << k, 1)

time: 26.6 us -> 25.2 us (0.947)
  Pallas kernels: 25.8 us -> 24.4 us
    pallas_call x1, Pallas kernels: 23.9 us -> 22.5 us  [body(): pl.pallas_call(functools.partial(kernel, nd, first, owners, spread, drive...]
where the time goes in v3:
time: 25.2 us; the launch traced here: 25.1 us
  Pallas kernels  24.4 us (97%)
  between operations  0.64 us (3%)
    pallas_call x1, Pallas kernels, body(): pl.pallas_call(functools.partial(kernel, nd, first, owners, spread, drive...  22.5 us
    pallas_call x1, Pallas kernels, body(): pl.pallas_call(functools.partial(finish, nd * rows * width), out_shape=(w...  1.93 us

profile of v3, /device:TPU:0, one launch (start us, length us, event | category | flops | bytes accessed | tf_op | source)
XLA Modules:
  0.0 25.1 jit_solution(18076854258056994787)
XLA Ops:
  0.6 22.5 %shard_map.59 = (f32[16,4096]{1,0:T(8,128)}, f32[16,4096]{1,0:T(8,128)}, f32[16,4096]{1,0:T(8,128)}, f32[2,4096]{1,0:T(2,128)}, f32[16,2,256]{2,1,0:T(2,128)}) custom-call(f32[32,16,4096]{2,1,0:T(8,128)} %hist.1, f32[16,4096]{1,0:T(8,128)} %src.1, f32[16,4096]{1,0:T(8,128)} %dif.1, f32[16,4096]{1,0:T(8,128)} %tgt.1), custom_call_target="tpu_custom_call" | custom-call | tf_op jit(solution)/shard_map/pallas_call | solution.py:352
  23.2 1.9 %shard_map.60 = (f32[16,4096]{1,0:T(8,128)}, f32[2]{0:T(128)}) custom-call(f32[16,4096]{1,0:T(8,128)} %get-tuple-element.7.free, f32[16,4096]{1,0:T(8,128)} %get-tuple-element.8.a, f32[16,4096]{1,0:T(8,128)} %get-tuple-element.9.b, f32[2,4096]{1,0:T(2,128)} %get-tuple-element.10.xr, f32[16,2,256]{2,1,0:T(2,128)} %get-tuple-element.11.tr), custom_call_target="tpu_custom_call" | custom-call | tf_op jit(solution)/shard_map/pallas_call | solution.py:372
